TPU v7x, 32 devices: a whole 2x2x4 slice. The times are simulated.
32 devices in a mesh: row: 8 (over y, x, core), col: 4 (over z).
Axes of the slice: x: 2, y: 2, z: 4, core: 2. Of those that a mesh axis runs over, the one named last changes fastest.
Arguments:
- features: bfloat16 [32768, 512], P('col', 'row'), may hold values from -6 to 6
- weight_t: bfloat16 [512, 512], P(None, 'row'), may hold values from -0.25 to 0.25
- tiles: bfloat16 [8192, 128, 128], P(('row', 'col')), may hold values from -0.15625 to 0.15625
- coords: int32 [2, 8192], P(None, ('row', 'col')), may hold values from 0 to 63, as said below
- counts: int32 [32], P(('row', 'col')), may hold values from 32 to 256, as said below
Outputs:
- output: bfloat16 [32768, 512], P('row', 'col')
Inputs may be any that keep to these rules, and one draw needn't show every extreme that they name: coords[0] of a slot lies in 0 to 31 and coords[1] in 0 to 63; the live slots of one grid cell name distinct tiles. `counts`: some grid cell has all 256 slots live in every draw.
All inputs are finite; a program needn't handle non-finite values.
Results may differ from a plain program's by a relative error of at most 0.0095.
Values may be sent and summed in bfloat16 or wider, within the bound.
A program may use at most 128 MiB of HBM per device.

v0:
```python
import functools

import jax
import jax.numpy as jnp
from jax import lax
from jax.experimental import pallas as pl
from jax.experimental.pallas import tpu as pltpu
from jax.sharding import PartitionSpec as P

TROW = 32
GATHER_PIECES = 8
REDUCE_PIECES = 8
BUNCH = 4
VMEM_LIMIT = 62 * 1024 * 1024


def swapped(p):
    return p + ((p // 2) % 2) * (1 - 2 * (p % 2))


def remote(src, dst, send, recv, axis, to):
    return pltpu.make_async_remote_copy(
        src_ref=src,
        dst_ref=dst,
        send_sem=send,
        recv_sem=recv,
        device_id={axis: to},
        device_id_type=pl.DeviceIdType.MESH,
    )


def gather_kernel(pairs, f_ref, w_ref, panel_ref, half_f, half_w,
                  pre_send, pre_recv, send_sem, recv_sem, sib_send, sib_recv):
    me = lax.axis_index("row")
    core = me % 2
    place = swapped(me // 2)
    sibling = me + 1 - 2 * core
    right = 2 * swapped(lax.rem(place + 1, pairs)) + core
    left = 2 * swapped(lax.rem(place + pairs - 1, pairs)) + core
    nodes = half_f.shape[1]
    outs = half_w.shape[1]
    thick = (nodes + outs) // GATHER_PIECES
    half = GATHER_PIECES // 2

    barrier = pltpu.get_barrier_semaphore()
    for other in (sibling, right, left):
        pl.semaphore_signal(
            barrier, inc=1, device_id={"row": other}, device_id_type=pl.DeviceIdType.MESH
        )
    pl.semaphore_wait(barrier, 3)

    theirs = 1 - core
    pre = [
        remote(f_ref.at[:, pl.ds(pl.multiple_of(theirs * nodes, nodes), nodes)], half_f,
               pre_send.at[0], pre_recv.at[0], "row", sibling),
        remote(w_ref.at[:, pl.ds(pl.multiple_of(theirs * outs, outs), outs)], half_w,
               pre_send.at[1], pre_recv.at[1], "row", sibling),
    ]
    for copy in pre:
        copy.start()
    for copy in pre:
        copy.wait()
    pair = me // 2

    def pack(mine_ref, other_ref, count, base):
        step = min(count, 512)
        for at in range(0, count, step):
            own = mine_ref[:, pl.ds(pl.multiple_of(core * count + at, step), step)]
            other = other_ref[:, at:at + step]
            first = jnp.where(core == 0, own, other)
            second = jnp.where(core == 0, other, own)
            panel_ref[pair, core, base + at:base + at + step] = jnp.concatenate([first, second], axis=0).T

    pack(f_ref, half_f, nodes, 0)
    pack(w_ref, half_w, outs, nodes)

    sends = []

    def piece(position, index):
        return panel_ref.at[swapped(position), core, pl.ds(index * thick, thick)]

    def along(way, distance, position, index, to):
        ref = piece(position, index)
        return remote(ref, ref, send_sem.at[way, distance, index],
                      recv_sem.at[way, distance, index], "row", to)

    sib_at = [0]

    def share(position, index):
        ref = piece(position, index)
        copy = remote(ref, ref, sib_send.at[sib_at[0]], sib_recv.at[sib_at[0]], "row", sibling)
        sib_at[0] += 1
        copy.start()
        sends.append(copy)

    longest = pairs // 2

    def carried(way, distance):
        indices = list(range(GATHER_PIECES)) if way == 0 else list(range(half, GATHER_PIECES)) + list(range(half))
        return indices if distance < longest else indices[:half]

    def start(way, distance, position, index):
        copy = along(way, distance, position, index, right if way == 0 else left)
        copy.start()
        return copy

    issued = []
    for i in range(GATHER_PIECES):
        for way in range(2):
            issued.append(start(way, 0, place, carried(way, 0)[i]))
    for i in range(GATHER_PIECES):
        share(place, i)
    for distance in range(1, longest + 1):
        from_left = lax.rem(place + pairs - distance, pairs)
        from_right = lax.rem(place + distance, pairs)
        for i in range(len(carried(0, distance))):
            for way, position in ((0, from_left), (1, from_right)):
                index = carried(way, distance)[i]
                along(way, distance - 1, position, index, right).wait_recv()
                if distance < longest and index in carried(way, distance + 1):
                    issued.append(start(way, distance, position, index))
                share(position, index)
    for copy in issued:
        copy.wait_send()
    for copy in sends:
        copy.wait()


def gather(features, weight_t, pairs):
    width, nodes = features.shape
    outs = weight_t.shape[1]
    rows = (nodes + outs) // 2
    longest = pairs // 2
    return pl.pallas_call(
        functools.partial(gather_kernel, pairs),
        out_shape=jax.ShapeDtypeStruct((pairs, 2, rows, 2 * width), features.dtype),
        in_specs=[pl.BlockSpec(memory_space=pltpu.VMEM)] * 2,
        out_specs=pl.BlockSpec(memory_space=pltpu.VMEM),
        scratch_shapes=[
            pltpu.VMEM((width, nodes // 2), features.dtype),
            pltpu.VMEM((width, outs // 2), features.dtype),
            pltpu.SemaphoreType.DMA((2,)),
            pltpu.SemaphoreType.DMA((2,)),
            pltpu.SemaphoreType.DMA((2, longest, GATHER_PIECES)),
            pltpu.SemaphoreType.DMA((2, longest, GATHER_PIECES)),
            pltpu.SemaphoreType.DMA((pairs * GATHER_PIECES,)),
            pltpu.SemaphoreType.DMA((pairs * GATHER_PIECES,)),
        ],
        compiler_params=pltpu.CompilerParams(
            collective_id=0, has_side_effects=True, vmem_limit_bytes=VMEM_LIMIT
        ),
        name="gather",
    )(features, weight_t)


def spread_kernel(nodes, coords_ref, counts_ref, panel_hbm, tiles_hbm, out_ref,
                  panel_ref, tiles_ref, total, total_low, weight, listed, where_from, lengths, sems):
    maxt, tile, _ = tiles_hbm.shape
    pairs = panel_ref.shape[0]
    here = nodes // tile
    room = listed.shape[0] // TROW
    count = counts_ref[0]
    copies = [
        pltpu.make_async_copy(panel_hbm, panel_ref, sems.at[0]),
        pltpu.make_async_copy(tiles_hbm, tiles_ref.at[pl.ds(0, maxt)], sems.at[1]),
    ]
    for copy in copies:
        copy.start()

    tiles_ref[maxt] = jnp.zeros((tile, tile), tiles_ref.dtype)

    def clear(row, carry):
        lengths[row] = 0
        return carry

    lax.fori_loop(0, TROW, clear, 0)

    def enter(slot, carry):
        row = coords_ref[0, slot]
        length = lengths[row]
        listed[row * room + length] = slot
        where_from[row * room + length] = coords_ref[1, slot]
        lengths[row] = length + 1
        return carry

    lax.fori_loop(0, count, enter, 0)

    def fill(row, carry):
        for k in range(BUNCH - 1):
            listed[row * room + lengths[row] + k] = maxt
            where_from[row * room + lengths[row] + k] = 0
        return carry

    lax.fori_loop(0, TROW, fill, 0)
    for copy in copies:
        copy.wait()

    outs = weight.shape[0] // 2
    for h in range(2):
        weight[h * outs:(h + 1) * outs, :] = jnp.concatenate(
            [panel_ref[q, h, nodes:, :] for q in range(pairs)], axis=1
        )

    def one_row(row, carry):
        def bunch(i, inner):
            left, right = [], []
            for k in range(BUNCH):
                at = row * room + i * BUNCH + k
                col = where_from[at]
                span = pl.ds(pl.multiple_of((col % here) * tile, tile), tile)
                left.append(tiles_ref[listed[at]])
                right.append(jnp.concatenate(
                    [panel_ref[q, col // here, span, :] for q in range(pairs)], axis=1))
            total[...] += jnp.dot(
                jnp.concatenate(left, axis=1), jnp.concatenate(right, axis=0),
                preferred_element_type=jnp.float32,
            )
            return inner

        total[...] = jnp.zeros_like(total)
        lax.fori_loop(0, (lengths[row] + BUNCH - 1) // BUNCH, bunch, 0)
        total_low[pl.ds(pl.multiple_of(row * tile, tile), tile), :] = total[...].astype(total_low.dtype)
        return carry

    lax.fori_loop(0, TROW, one_row, 0)
    parts, rows, width = out_ref.shape
    block = 512

    def finish(i, carry):
        at = pl.ds(pl.multiple_of(i * block, block), block)
        result = lax.dot_general(
            total_low[at, :], weight[...],
            (((1,), (1,)), ((), ())), preferred_element_type=jnp.float32,
        ).astype(out_ref.dtype)
        for d in range(parts):
            out_ref[d, at, :] = result[:, d * width:(d + 1) * width]
        return carry

    lax.fori_loop(0, rows // block, finish, 0)


def spread(coords, counts, panel, tiles, outs, parts):
    maxt, tile, _ = tiles.shape
    pairs, _, rows, wide = panel.shape
    nodes = rows - outs // 2
    feat = pairs * wide
    room = 2 * nodes // tile + BUNCH
    return pl.pallas_call(
        functools.partial(spread_kernel, nodes),
        out_shape=jax.ShapeDtypeStruct((parts, TROW * tile, outs // parts), jnp.bfloat16),
        in_specs=[
            pl.BlockSpec(memory_space=pltpu.SMEM),
            pl.BlockSpec(memory_space=pltpu.SMEM),
            pl.BlockSpec(memory_space=pl.ANY),
            pl.BlockSpec(memory_space=pl.ANY),
        ],
        out_specs=pl.BlockSpec(memory_space=pltpu.VMEM),
        scratch_shapes=[
            pltpu.VMEM(panel.shape, panel.dtype),
            pltpu.VMEM((maxt + 1, tile, tile), tiles.dtype),
            pltpu.VMEM((tile, feat), jnp.float32),
            pltpu.VMEM((TROW * tile, feat), jnp.bfloat16),
            pltpu.VMEM((outs, feat), jnp.bfloat16),
            pltpu.SMEM((TROW * room,), jnp.int32),
            pltpu.SMEM((TROW * room,), jnp.int32),
            pltpu.SMEM((TROW,), jnp.int32),
            pltpu.SemaphoreType.DMA((2,)),
        ],
        compiler_params=pltpu.CompilerParams(vmem_limit_bytes=VMEM_LIMIT),
        name="spread",
    )(coords, counts, panel, tiles)


def reduce_kernel(parts, part_ref, out_ref, slots, send_sem, recv_sem):
    me = lax.axis_index("col")
    right = lax.rem(me + 1, parts)
    left = lax.rem(me + parts - 1, parts)
    rows = part_ref.shape[1]
    thick = rows // 2 // REDUCE_PIECES

    barrier = pltpu.get_barrier_semaphore()
    for other in (right, left):
        pl.semaphore_signal(
            barrier, inc=1, device_id={"col": other}, device_id_type=pl.DeviceIdType.MESH
        )
    pl.semaphore_wait(barrier, 2)

    def aim(way, step):
        return lax.rem(me + parts - 1 - step, parts) if way == 0 else lax.rem(me + 1 + step, parts)

    def mine(way, step, index):
        return part_ref.at[aim(way, step), pl.ds(way * (rows // 2) + index * thick, thick)]

    def slot(way, step, index):
        return slots.at[way, step, pl.ds(index * thick, thick)]

    def move(way, step, index):
        source = mine(way, 0, index) if step == 0 else slot(way, step - 1, index)
        return remote(source, slot(way, step, index), send_sem.at[way, step, index],
                      recv_sem.at[way, step, index], "col", right if way == 0 else left)

    issued = []
    for index in range(REDUCE_PIECES):
        for way in range(2):
            copy = move(way, 0, index)
            copy.start()
            issued.append(copy)
    held = None
    for step in range(parts - 1):
        for index in range(REDUCE_PIECES):
            for way in range(2):
                move(way, step, index).wait_recv()
                arrived = slot(way, step, index)
                added = (arrived[...].astype(jnp.float32)
                         + mine(way, step + 1, index)[...].astype(jnp.float32)).astype(out_ref.dtype)
                if step < parts - 2:
                    arrived[...] = added
                else:
                    out_ref[pl.ds(way * (rows // 2) + index * thick, thick)] = added
                if held is not None:
                    held.start()
                    issued.append(held)
                    held = None
                if step < parts - 2:
                    held = move(way, step + 1, index)
    for copy in issued:
        copy.wait_send()


def reduce(part):
    parts, rows, width = part.shape
    return pl.pallas_call(
        functools.partial(reduce_kernel, parts),
        out_shape=jax.ShapeDtypeStruct((rows, width), part.dtype),
        in_specs=[pl.BlockSpec(memory_space=pltpu.VMEM)],
        out_specs=pl.BlockSpec(memory_space=pltpu.VMEM),
        scratch_shapes=[
            pltpu.VMEM((2, parts - 1, rows // 2, width), part.dtype),
            pltpu.SemaphoreType.DMA((2, parts - 1, REDUCE_PIECES)),
            pltpu.SemaphoreType.DMA((2, parts - 1, REDUCE_PIECES)),
        ],
        compiler_params=pltpu.CompilerParams(
            collective_id=1, has_side_effects=True, vmem_limit_bytes=VMEM_LIMIT
        ),
        name="reduce",
    )(part)


def solution(mesh):
    placed = (
        P("col", "row"),
        P(None, "row"),
        P(("row", "col"), None, None),
        P(None, ("row", "col")),
        P(("row", "col")),
    )
    pairs = mesh.shape["row"] // 2
    parts = mesh.shape["col"]

    def body(features, weight_t, tiles, coords, counts):
        panel = gather(features.T, weight_t.T, pairs)
        part = spread(coords, counts, panel, tiles, weight_t.shape[0], parts)
        return reduce(part)

    return jax.shard_map(
        body, mesh=mesh, in_specs=placed, out_specs=P("row", "col"), check_vma=False
    )
```

profile of v0, /device:TPU:4, one launch (start us, length us, event | category | flops | bytes accessed | tf_op | source)
XLA Modules:
  0.0 159.0 jit_solution(1096233162306913533)
XLA Ops:
  0.7 48.0 %gather.1.panel_hbm = bf16[4,2,4352,128]{3,2,1,0:T(8,128)(2,1)} custom-call(bf16[64,8192]{1,0:T(8,128)(2,1)} %bitcast.2, bf16[64,512]{1,0:T(8,128)(2,1)} %bitcast.3), custom_call_target="tpu_custom_call" | custom-call | tf_op jit(solution)/shard_map/gather/pallas_call | solution.py:134
  48.7 20.1 %spread.1.part_ref = bf16[4,4096,128]{2,1,0:T(8,128)(2,1)} custom-call(s32[2,256]{1,0:T(2,128)} %coords_ref.1, s32[1]{0:T(128)S(6)} %copy.7.counts_ref, bf16[4,2,4352,128]{3,2,1,0:T(8,128)(2,1)} %gather.1.panel_hbm, bf16[256,128,128]{2,1,0:T(8,128)(2,1)} %tiles_hbm.1), custom_call_target="tpu_custom_call" | custom-call | tf_op jit(solution)/shard_map/spread/pallas_call | solution.py:248
  68.9 87.9 %reduce.1 = bf16[4096,128]{1,0:T(8,128)(2,1)} custom-call(bf16[4,4096,128]{2,1,0:T(8,128)(2,1)} %spread.1.part_ref), custom_call_target="tpu_custom_call" | custom-call | tf_op jit(solution)/shard_map/reduce/pallas_call | solution.py:332
  156.7 2.3 %copy.8 = bf16[4096,128]{1,0:T(8,128)(2,1)} copy(bf16[4096,128]{1,0:T(8,128)(2,1)} %reduce.1) | data formatting | bytes 2097152
where the time goes:
time: 159 us
  Pallas kernels  156 us (98%)
  local copies, waits for them, and re-layouts  2.26 us (1%)
    pallas_call x1, Pallas kernels, reduce(): pl.pallas_call(functools.partial(reduce_kernel, parts), out_shape=jax.Sha...  87.9 us
    pallas_call x1, Pallas kernels, gather(): pl.pallas_call(functools.partial(gather_kernel, pairs), out_shape=jax.Sha...  48 us
    pallas_call x1, Pallas kernels, spread(): pl.pallas_call(functools.partial(spread_kernel, nodes), out_shape=jax.Sha...  20.1 us

commit v1 on v0

v1 whole, which is shorter than its diff:
```python
import functools

import jax
import jax.numpy as jnp
from jax import lax
from jax.experimental import pallas as pl
from jax.experimental.pallas import tpu as pltpu
from jax.sharding import PartitionSpec as P

BUNCH = 4
PIECES = 8
EARLY = 2
VMEM_LIMIT = 62 * 1024 * 1024


def remote(src, dst, send, recv, axis, to):
    return pltpu.make_async_remote_copy(
        src_ref=src,
        dst_ref=dst,
        send_sem=send,
        recv_sem=recv,
        device_id={axis: to},
        device_id_type=pl.DeviceIdType.MESH,
    )


def plan_kernel(coords_ref, counts_ref, slots_ref, cols_ref, keep_ref, last_ref, lengths, bases):
    maxt = coords_ref.shape[1]
    trow = last_ref.shape[0]
    bunches = keep_ref.shape[0] - 1
    count = counts_ref[0]

    def clear_row(row, carry):
        lengths[row] = 0
        return carry

    lax.fori_loop(0, trow, clear_row, 0)

    def clear_slot(at, carry):
        slots_ref[at] = maxt
        cols_ref[at] = 0
        return carry

    lax.fori_loop(0, slots_ref.shape[0], clear_slot, 0, unroll=8)

    def clear_start(at, carry):
        keep_ref[at] = 1.0
        return carry

    lax.fori_loop(0, bunches, clear_start, 0, unroll=8)

    def tally(slot, carry):
        row = coords_ref[0, slot]
        lengths[row] = lengths[row] + 1
        return carry

    lax.fori_loop(0, count, tally, 0)

    def lay(row, base):
        need = (lengths[row] + BUNCH - 1) // BUNCH
        bases[row] = base * BUNCH
        keep_ref[jnp.where(need > 0, base, bunches)] = 0.0
        last_ref[row] = jnp.where(need > 0, base + need - 1, bunches)
        return base + need

    lax.fori_loop(0, trow, lay, 0)

    def enter(slot, carry):
        row = coords_ref[0, slot]
        at = bases[row]
        slots_ref[at] = slot
        cols_ref[at] = coords_ref[1, slot]
        bases[row] = at + 1
        return carry

    lax.fori_loop(0, count, enter, 0)


def plan(coords, counts, trow, bunches):
    smem = pl.BlockSpec(memory_space=pltpu.SMEM)
    return pl.pallas_call(
        plan_kernel,
        out_shape=[
            jax.ShapeDtypeStruct((bunches * BUNCH,), jnp.int32),
            jax.ShapeDtypeStruct((bunches * BUNCH,), jnp.int32),
            jax.ShapeDtypeStruct((bunches + 1,), jnp.float32),
            jax.ShapeDtypeStruct((trow,), jnp.int32),
        ],
        in_specs=[smem] * 2,
        out_specs=[smem] * 4,
        scratch_shapes=[pltpu.SMEM((trow,), jnp.int32), pltpu.SMEM((trow,), jnp.int32)],
        name="plan",
    )(coords, counts)


def layer_kernel(rows_n, parts, slots_ref, cols_ref, keep_ref, last_ref, f_ref, w_ref, tiles_hbm, out_ref,
                 tiles_ref, ft, xs, w_mine, weights, panels, runs, partial, landed,
                 tiles_sem, f_send, f_recv, w_send, w_recv, h_send, h_recv, sib_send, z_send, z_recv):
    me = lax.axis_index("row")
    here = lax.axis_index("col")
    maxt, tile, _ = tiles_hbm.shape
    fw, nodes = f_ref.shape
    block = nodes // rows_n
    deep = block // tile
    width = out_ref.shape[1]
    rows = out_ref.shape[0]
    feat = rows_n * fw
    bunches = keep_ref.shape[0] - 1
    trow = last_ref.shape[0]
    core = me % 2
    sibling = me + 1 - 2 * core
    twins = rows_n // 2

    fetch = pltpu.make_async_copy(tiles_hbm, tiles_ref.at[pl.ds(0, maxt)], tiles_sem)
    fetch.start()

    barrier = pltpu.get_barrier_semaphore()
    for step in range(1, rows_n):
        pl.semaphore_signal(barrier, inc=1, device_id={"row": lax.rem(me + step, rows_n)},
                            device_id_type=pl.DeviceIdType.MESH)

    @pl.when(here > 0)
    def _():
        pl.semaphore_signal(barrier, inc=1, device_id={"col": here - 1}, device_id_type=pl.DeviceIdType.MESH)

    @pl.when(here < parts - 1)
    def _():
        pl.semaphore_signal(barrier, inc=1, device_id={"col": here + 1}, device_id_type=pl.DeviceIdType.MESH)

    beside = jnp.where(here > 0, 1, 0) + jnp.where(here < parts - 1, 1, 0)
    pl.semaphore_wait(barrier, rows_n - 1 + beside)

    low_half = here < parts - 1 - here
    few = jnp.minimum(here, parts - 1 - here)
    order = []
    for k in range(parts - 1):
        step = jnp.where(k < 2 * few, k // 2, k - few)
        first = jnp.where(k < 2 * few, k % 2, 0) == 0
        order.append(jnp.where(first == low_half, parts - 1 - step, step))
    order.append(here)

    for q in range(parts):
        w_mine[q] = w_ref[:, q * width:(q + 1) * width]

    issued = []

    def begin(copy):
        copy.start()
        issued.append(copy)

    def send_weight(k):
        for step in range(1, rows_n):
            begin(remote(w_mine.at[order[k]], weights[k].at[pl.ds(pl.multiple_of(me * fw, fw), fw)],
                         w_send.at[k, step], w_recv.at[k, me], "row", lax.rem(me + step, rows_n)))

    send_weight(0)
    for step in range(1, rows_n):
        to = lax.rem(me + step, rows_n)
        begin(remote(f_ref.at[:, pl.ds(pl.multiple_of(to * block, block), block)],
                     ft.at[pl.ds(pl.multiple_of(me * fw, fw), fw)],
                     f_send.at[step], f_recv.at[me], "row", to))
    for k in range(1, EARLY):
        send_weight(k)

    mine = pl.ds(pl.multiple_of(me * fw, fw), fw)
    ft[mine, :] = f_ref[:, pl.ds(pl.multiple_of(me * block, block), block)]
    for k in range(parts):
        weights[k][mine, :] = w_mine[order[k]]

    tiles_ref[maxt] = jnp.zeros((tile, tile), tiles_ref.dtype)
    runs[bunches] = jnp.zeros((tile, width), runs.dtype)

    def weight_in(k):
        for step in range(1, rows_n):
            at = lax.rem(me + step, rows_n)
            place = weights[k].at[pl.ds(pl.multiple_of(at * fw, fw), fw)]
            remote(place, place, w_send.at[k, step], w_recv.at[k, at], "row", at).wait_recv()

    for step in range(1, rows_n):
        at = lax.rem(me + step, rows_n)
        place = ft.at[pl.ds(pl.multiple_of(at * fw, fw), fw)]
        remote(place, place, f_send.at[step], f_recv.at[at], "row", at).wait_recv()
    strip = min(block, 512)
    for low in range(0, feat, tile):
        for at in range(0, block, strip):
            xs[at:at + strip, low:low + tile] = ft[low:low + tile, at:at + strip].T

    def spot(k, at):
        return panels[k].at[pl.ds(at * deep, deep)]

    def share(k):
        weight_in(k)
        product = jnp.dot(xs[...], weights[k][...], preferred_element_type=jnp.float32)
        panels[k][pl.ds(me * deep, deep)] = product.astype(panels[k].dtype).reshape(deep, tile, width)
        for step in range(1, twins):
            begin(remote(spot(k, me), spot(k, me), h_send.at[k, step], h_recv.at[k, me], "row",
                         lax.rem(me + 2 * step, rows_n)))
        begin(remote(spot(k, me), spot(k, me), h_send.at[k, 0], h_recv.at[k, me], "row", sibling))

    for k in range(EARLY):
        share(k)
    for k in range(EARLY, parts):
        send_weight(k)
    fetch.wait()

    def collect(k):
        for step in range(1, twins):
            at = lax.rem(me + 2 * step, rows_n)
            remote(spot(k, at), spot(k, at), sib_send.at[k, step], h_recv.at[k, at], "row", sibling).wait_recv()
            begin(remote(spot(k, at), spot(k, at), sib_send.at[k, step], h_recv.at[k, at], "row", sibling))
        for step in range(twins):
            at = lax.rem(sibling + 2 * step, rows_n)
            remote(spot(k, at), spot(k, at), sib_send.at[k, step], h_recv.at[k, at], "row", sibling).wait_recv()

    def multiply(k):
        panel = panels[k]

        def bunch(i, total):
            left, right = [], []
            for j in range(BUNCH):
                at = i * BUNCH + j
                left.append(tiles_ref[slots_ref[at]])
                right.append(panel[cols_ref[at]])
            here_sum = jnp.dot(jnp.concatenate(left, axis=1), jnp.concatenate(right, axis=0),
                               preferred_element_type=jnp.float32)
            total = total * keep_ref[i] + here_sum
            runs[i] = total.astype(runs.dtype)
            return total

        lax.fori_loop(0, bunches, bunch, jnp.zeros((tile, width), jnp.float32))
        for row in range(trow):
            partial[k, row * tile:(row + 1) * tile, :] = runs[last_ref[row]]

    thick = rows // PIECES

    def piece(ref, which, p):
        return ref.at[which, pl.ds(p * thick, thick)]

    def stream(k):
        q = order[k]
        up = q > here
        inner = (here > 0) & (here < parts - 1)
        to = jnp.where(up, here + 1, here - 1)
        slot = jnp.where(q == here - 1, parts, q)
        for p in range(PIECES):
            @pl.when(inner)
            def _():
                remote(piece(landed, q, p), piece(landed, q, p), z_send.at[k, p], z_recv.at[q, p],
                       "col", to).wait_recv()
                partial[k, p * thick:(p + 1) * thick, :] = (
                    partial[k, p * thick:(p + 1) * thick, :].astype(jnp.float32)
                    + landed[q, p * thick:(p + 1) * thick, :].astype(jnp.float32)).astype(partial.dtype)

            begin(remote(piece(partial, k, p), piece(landed, slot, p), z_send.at[k, p], z_recv.at[slot, p],
                         "col", to))

    for k in range(parts - 1):
        collect(k)
        multiply(k)
        stream(k)
        if k == 0:
            for later in range(EARLY, parts):
                share(later)
    own = parts - 1
    collect(own)
    multiply(own)
    for p in range(PIECES):
        span = slice(p * thick, (p + 1) * thick)
        for side, slot, there in ((0, here, here > 0), (1, parts, here < parts - 1)):
            @pl.when(there)
            def _():
                remote(piece(landed, slot, p), piece(landed, slot, p), z_send.at[own, p], z_recv.at[slot, p],
                       "col", here).wait_recv()

        total = partial[own, span, :].astype(jnp.float32)
        total = total + jnp.where(here > 0, landed[here, span, :].astype(jnp.float32), 0.0)
        total = total + jnp.where(here < parts - 1, landed[parts, span, :].astype(jnp.float32), 0.0)
        out_ref[span, :] = total.astype(out_ref.dtype)
    for copy in issued:
        copy.wait_send()


def layer(lists, features, weight_t, tiles, rows_n, parts):
    maxt, tile, _ = tiles.shape
    fw, nodes = features.shape
    outs = weight_t.shape[1]
    width = outs // parts
    feat = fw * rows_n
    block = nodes // rows_n
    trow = lists[3].shape[0]
    rows = trow * tile
    bunches = lists[2].shape[0] - 1
    kind = features.dtype
    smem = pl.BlockSpec(memory_space=pltpu.SMEM)
    vmem = pl.BlockSpec(memory_space=pltpu.VMEM)
    dma = pltpu.SemaphoreType.DMA
    return pl.pallas_call(
        functools.partial(layer_kernel, rows_n, parts),
        out_shape=jax.ShapeDtypeStruct((rows, width), kind),
        in_specs=[smem] * 4 + [vmem, vmem, pl.BlockSpec(memory_space=pl.ANY)],
        out_specs=vmem,
        scratch_shapes=[
            pltpu.VMEM((maxt + 1, tile, tile), kind),
            pltpu.VMEM((feat, block), kind),
            pltpu.VMEM((block, feat), kind),
            pltpu.VMEM((parts, fw, width), kind),
            [pltpu.VMEM((feat, width), kind) for _ in range(parts)],
            [pltpu.VMEM((nodes // tile, tile, width), kind) for _ in range(parts)],
            pltpu.VMEM((bunches + 1, tile, width), kind),
            pltpu.VMEM((parts, rows, width), kind),
            pltpu.VMEM((parts + 1, rows, width), kind),
            dma,
            dma((rows_n,)),
            dma((rows_n,)),
            dma((parts, rows_n)),
            dma((parts, rows_n)),
            dma((parts, rows_n)),
            dma((parts, rows_n)),
            dma((parts, rows_n)),
            dma((parts, PIECES)),
            dma((parts + 1, PIECES)),
        ],
        compiler_params=pltpu.CompilerParams(
            collective_id=0, has_side_effects=True, vmem_limit_bytes=VMEM_LIMIT
        ),
        name="layer",
    )(*lists, features, weight_t, tiles)


def solution(mesh):
    placed = (
        P("col", "row"),
        P(None, "row"),
        P(("row", "col"), None, None),
        P(None, ("row", "col")),
        P(("row", "col")),
    )
    rows_n = mesh.shape["row"]
    parts = mesh.shape["col"]

    def body(features, weight_t, tiles, coords, counts):
        maxt, tile, _ = tiles.shape
        trow = features.shape[0] * parts // rows_n // tile
        bunches = (maxt + trow * (BUNCH - 1)) // BUNCH
        lists = plan(coords, counts, trow, bunches)
        return layer(lists, features.T, weight_t.T, tiles, rows_n, parts)

    return jax.shard_map(
        body, mesh=mesh, in_specs=placed, out_specs=P("row", "col"), check_vma=False
    )
```

time: 159 us -> 151 us (0.950)
  the two profiles are of different devices: /device:TPU:4 before, /device:TPU:16 now
where the time goes in v1:
time: 151 us; the launch traced here: 149 us
  Pallas kernels  146 us (97%)
  local copies, waits for them, and re-layouts  2.26 us (1%)
    pallas_call x1, Pallas kernels, layer(): pl.pallas_call(functools.partial(layer_kernel, rows_n, parts), out_shape=...  142 us
    pallas_call x1, Pallas kernels, plan(): pl.pallas_call(plan_kernel, out_shape=[jax.ShapeDtypeStruct((bunches * BU...  4.34 us

profile of v1, /device:TPU:16, one launch (start us, length us, event | category | flops | bytes accessed | tf_op | source)
XLA Modules:
  0.0 149.4 jit_solution(14966819698335628328)
XLA Ops:
  0.7 4.3 %plan.1 = (s32[352]{0:T(512)}, s32[352]{0:T(512)}, f32[89]{0:T(128)}, s32[32]{0:T(128)}) custom-call(s32[2,256]{1,0:T(2,128)} %coords_ref.1, s32[1]{0:T(128)S(6)} %copy.7.counts_ref), custom_call_target="tpu_custom_call" | custom-call | tf_op jit(solution)/shard_map/plan/pallas_call | solution.py:81
  5.0 142.1 %layer.1 = bf16[4096,128]{1,0:T(8,128)(2,1)} custom-call(s32[352]{0:T(512)} %get-tuple-element.9.slots_ref, s32[352]{0:T(512)} %get-tuple-element.10.cols_ref, f32[89]{0:T(128)} %get-tuple-element.11.keep_ref, s32[32]{0:T(128)} %get-tuple-element.12.last_ref, bf16[64,8192]{1,0:T(8,128)(2,1)} %bitcast.2, bf16[64,512]{1,0:T(8,128)(2,1)} %bitcast.3, ...), custom_call_target="tpu_custom_call" | custom-call | tf_op jit(solution)/shard_map/layer/pallas_call | solution.py:297
  147.1 2.3 %copy.8 = bf16[4096,128]{1,0:T(8,128)(2,1)} copy(bf16[4096,128]{1,0:T(8,128)(2,1)} %layer.1) | data formatting | bytes 2097152

commit v2 on v1

v2 whole, which is shorter than its diff:
```python
import functools

import jax
import jax.numpy as jnp
from jax import lax
from jax.experimental import pallas as pl
from jax.experimental.pallas import tpu as pltpu
from jax.sharding import PartitionSpec as P

BUNCH = 2
UNROLL = 16
PIECES = 4
EARLY = 2
HALF = 64
VMEM_LIMIT = 62 * 1024 * 1024


def remote(src, dst, send, recv, axis, to):
    return pltpu.make_async_remote_copy(
        src_ref=src,
        dst_ref=dst,
        send_sem=send,
        recv_sem=recv,
        device_id={axis: to},
        device_id_type=pl.DeviceIdType.MESH,
    )


def plan(coords_ref, count, trow, lists_ref, keep_ref):
    maxt = coords_ref.shape[1]
    spots = lists_ref.shape[1]
    bunches = maxt // BUNCH + trow * (BUNCH - 1) // BUNCH
    lists_ref[...] = jnp.zeros(lists_ref.shape, jnp.int32)
    keep_ref[...] = jnp.zeros(keep_ref.shape, jnp.float32)

    def iota(shape, axis):
        return lax.broadcasted_iota(jnp.int32, shape, axis)

    def total(mask, value, axis):
        return jnp.sum(jnp.where(mask, value, 0), axis=axis, keepdims=True, dtype=jnp.int32)

    slot = iota((1, maxt), 1)
    row = jnp.where(slot < count, coords_ref[0:1, :], 2 * trow)
    square = jnp.broadcast_to(row, (maxt, maxt))
    turned = square.T
    rank = total((square == turned) & (iota((maxt, maxt), 0) < iota((maxt, maxt), 1)), 1, 0)

    def rounds(number):
        return (number + (BUNCH - 1)) // BUNCH

    match = iota((trow, maxt), 0) == row
    need_down = rounds(total(match, 1, 1))
    spot = iota((maxt, 128), 1)
    need_along = rounds(total(turned[:, :128] == spot, 1, 0))
    down = iota((trow, 128), 0)
    along = iota((trow, 128), 1)
    base_down = total(along < down, need_along, 1)
    base_along = total(down < along, need_down, 0)
    last = jnp.where(need_along > 0, base_along + need_along - 1, bunches)
    place = jnp.where(slot < count, rank + total(match, base_down * BUNCH, 0), -1)
    place_down = jnp.broadcast_to(place, (maxt, maxt)).T[:, :128]
    col_down = jnp.broadcast_to(coords_ref[1:2, :], (maxt, maxt)).T[:, :128]
    for low in range(0, spots, 128):
        hit = place_down == spot + low
        lists_ref[0:1, low:low + 128] = total(hit, iota((maxt, 128), 0) - maxt, 0) + maxt
        lists_ref[1:2, low:low + 128] = total(hit, col_down, 0)
        begins = total((base_down == along + low) & (need_down > 0), 1, 0)
        keep_ref[0:1, low:low + 128] = 1.0 - begins.astype(jnp.float32)
    lists_ref[2:3, 0:128] = jnp.where(slot[:, :128] < trow, last, 0)


def layer_kernel(rows_n, parts, count_ref, coords_ref, f_ref, w_ref, tiles_hbm, out_ref,
                 tiles_ref, ft, xs, w_mine, weights, panels, spread, runs, partial, landed,
                 lists_made, keep_made, lists_ref, keep_ref,
                 local_sem, f_send, f_recv, w_send, w_recv, h_send, h_recv, sib_send, z_send, z_recv):
    me = lax.axis_index("row")
    here = lax.axis_index("col")
    maxt, tile, _ = tiles_hbm.shape
    fw, nodes = f_ref.shape
    block = nodes // rows_n
    deep = block // tile // 2
    rows, width = out_ref.shape
    split = width // HALF
    chunks = parts * split
    feat = rows_n * fw
    bunches = runs.shape[0] - 1
    trow = rows // tile
    core = me % 2
    sibling = me + 1 - 2 * core
    twins = rows_n // 2

    fetch = pltpu.make_async_copy(tiles_hbm, tiles_ref.at[pl.ds(0, maxt)], local_sem.at[0])
    fetch.start()

    barrier = pltpu.get_barrier_semaphore()
    for step in range(1, rows_n):
        pl.semaphore_signal(barrier, inc=1, device_id={"row": lax.rem(me + step, rows_n)},
                            device_id_type=pl.DeviceIdType.MESH)

    @pl.when(here > 0)
    def _():
        pl.semaphore_signal(barrier, inc=1, device_id={"col": here - 1}, device_id_type=pl.DeviceIdType.MESH)

    @pl.when(here < parts - 1)
    def _():
        pl.semaphore_signal(barrier, inc=1, device_id={"col": here + 1}, device_id_type=pl.DeviceIdType.MESH)

    beside = jnp.where(here > 0, 1, 0) + jnp.where(here < parts - 1, 1, 0)
    pl.semaphore_wait(barrier, rows_n - 1 + beside)

    low_half = here < parts - 1 - here
    few = jnp.minimum(here, parts - 1 - here)
    order = []
    for k in range(parts - 1):
        step = jnp.where(k < 2 * few, k // 2, k - few)
        first = jnp.where(k < 2 * few, k % 2, 0) == 0
        order.append(jnp.where(first == low_half, parts - 1 - step, step))
    order.append(here)

    for q in range(parts):
        w_mine[q] = w_ref[:, q * width:(q + 1) * width]

    issued = []

    def begin(copy):
        copy.start()
        issued.append(copy)

    def send_weight(k):
        for step in range(1, rows_n):
            begin(remote(w_mine.at[order[k]], weights[k].at[pl.ds(pl.multiple_of(me * fw, fw), fw)],
                         w_send.at[k, step], w_recv.at[k, me], "row", lax.rem(me + step, rows_n)))

    send_weight(0)
    for step in range(1, rows_n):
        to = lax.rem(me + step, rows_n)
        begin(remote(f_ref.at[:, pl.ds(pl.multiple_of(to * block, block), block)],
                     ft.at[pl.ds(pl.multiple_of(me * fw, fw), fw)],
                     f_send.at[step], f_recv.at[me], "row", to))
    for k in range(1, EARLY):
        send_weight(k)

    mine = pl.ds(pl.multiple_of(me * fw, fw), fw)
    ft[mine, :] = f_ref[:, pl.ds(pl.multiple_of(me * block, block), block)]
    for k in range(parts):
        weights[k][mine, :] = w_mine[order[k]]

    tiles_ref[maxt] = jnp.zeros((tile, tile), tiles_ref.dtype)
    runs[bunches] = jnp.zeros((tile, tile), runs.dtype)
    plan(coords_ref, count_ref[0], trow, lists_made, keep_made)
    moves = [
        pltpu.make_async_copy(lists_made, lists_ref, local_sem.at[1]),
        pltpu.make_async_copy(keep_made, keep_ref, local_sem.at[2]),
    ]
    for move in moves:
        move.start()

    def weight_in(k):
        for step in range(1, rows_n):
            at = lax.rem(me + step, rows_n)
            place = weights[k].at[pl.ds(pl.multiple_of(at * fw, fw), fw)]
            remote(place, place, w_send.at[k, step], w_recv.at[k, at], "row", at).wait_recv()

    for step in range(1, rows_n):
        at = lax.rem(me + step, rows_n)
        place = ft.at[pl.ds(pl.multiple_of(at * fw, fw), fw)]
        remote(place, place, f_send.at[step], f_recv.at[at], "row", at).wait_recv()
    strip = min(block, 512)
    for low in range(0, feat, tile):
        for at in range(0, block, strip):
            xs[at:at + strip, low:low + tile] = ft[low:low + tile, at:at + strip].T

    def spot(c, at):
        return panels[c].at[pl.ds(at * deep, deep)]

    def share(k):
        weight_in(k)
        product = jnp.dot(xs[...], weights[k][...], preferred_element_type=jnp.float32).astype(xs.dtype)
        for h in range(split):
            c = k * split + h
            cut = product[:, h * HALF:(h + 1) * HALF]
            packed = jnp.concatenate([cut[:block // 2], cut[block // 2:]], axis=1)
            panels[c][pl.ds(me * deep, deep)] = packed.reshape(deep, tile, tile)
            for step in range(1, twins):
                begin(remote(spot(c, me), spot(c, me), h_send.at[c, step], h_recv.at[c, me], "row",
                             lax.rem(me + 2 * step, rows_n)))
            begin(remote(spot(c, me), spot(c, me), h_send.at[c, 0], h_recv.at[c, me], "row", sibling))

    for k in range(EARLY):
        share(k)
    for k in range(EARLY, parts):
        send_weight(k)
    fetch.wait()
    for move in moves:
        move.wait()

    def collect(c):
        for step in range(1, twins):
            at = lax.rem(me + 2 * step, rows_n)
            passed = remote(spot(c, at), spot(c, at), sib_send.at[c, step], h_recv.at[c, at], "row", sibling)
            passed.wait_recv()
            begin(passed)
        for step in range(twins):
            at = lax.rem(sibling + 2 * step, rows_n)
            remote(spot(c, at), spot(c, at), sib_send.at[c, step], h_recv.at[c, at], "row", sibling).wait_recv()

    def multiply(c):
        for at in range(rows_n * deep):
            both = panels[c][at]
            low = at // deep * 2 * deep + at % deep
            spread[low] = both
            spread[low + deep] = jnp.concatenate([both[:, HALF:], both[:, :HALF]], axis=1)

        def bunch(i, total):
            left, right = [], []
            for j in range(BUNCH):
                at = i * BUNCH + j
                left.append(tiles_ref[lists_ref[0, at]])
                right.append(spread[lists_ref[1, at]])
            part = jnp.dot(jnp.concatenate(left, axis=1), jnp.concatenate(right, axis=0),
                           preferred_element_type=jnp.float32)
            total = total * keep_ref[0, i] + part
            runs[i] = total.astype(runs.dtype)
            return total

        lax.fori_loop(0, bunches, bunch, jnp.zeros((tile, tile), jnp.float32), unroll=UNROLL)
        for row in range(trow // 2):
            low = runs[lists_ref[2, row]]
            high = runs[lists_ref[2, row + trow // 2]]
            partial[c, row * tile:(row + 1) * tile, :] = jnp.concatenate([low[:, :HALF], high[:, :HALF]], axis=1)

    thick = rows // 2 // PIECES

    def piece(ref, which, p):
        return ref.at[which, pl.ds(p * thick, thick)]

    def stream(c):
        q = order[c // split]
        up = q > here
        inner = (here > 0) & (here < parts - 1)
        to = jnp.where(up, here + 1, here - 1)
        came = q * split + c % split
        goes = jnp.where(q == here - 1, parts, q) * split + c % split
        for p in range(PIECES):
            span = slice(p * thick, (p + 1) * thick)

            @pl.when(inner)
            def _():
                remote(piece(landed, came, p), piece(landed, came, p), z_send.at[c, p], z_recv.at[came, p],
                       "col", to).wait_recv()
                partial[c, span, :] = (partial[c, span, :].astype(jnp.float32)
                                       + landed[came, span, :].astype(jnp.float32)).astype(partial.dtype)

            begin(remote(piece(partial, c, p), piece(landed, goes, p), z_send.at[c, p], z_recv.at[goes, p],
                         "col", to))

    for c in range(chunks - split):
        collect(c)
        multiply(c)
        stream(c)
        if c == 0:
            for later in range(EARLY, parts):
                share(later)
    for h in range(split):
        c = chunks - split + h
        collect(c)
        multiply(c)
    for p in range(PIECES):
        for h in range(split):
            span = slice(p * thick, (p + 1) * thick)
            c = chunks - split + h
            below = here * split + h
            above = parts * split + h
            for slot, there in ((below, here > 0), (above, here < parts - 1)):
                @pl.when(there)
                def _():
                    remote(piece(landed, slot, p), piece(landed, slot, p), z_send.at[c, p], z_recv.at[slot, p],
                           "col", here).wait_recv()

            total = partial[c, span, :].astype(jnp.float32)
            total = total + jnp.where(here > 0, landed[below, span, :].astype(jnp.float32), 0.0)
            total = total + jnp.where(here < parts - 1, landed[above, span, :].astype(jnp.float32), 0.0)
            total = total.astype(out_ref.dtype)
            high = slice(rows // 2 + p * thick, rows // 2 + (p + 1) * thick)
            out_ref[span, h * HALF:(h + 1) * HALF] = total[:, :HALF]
            out_ref[high, h * HALF:(h + 1) * HALF] = total[:, HALF:]
    for copy in issued:
        copy.wait_send()


def layer(features, weight_t, tiles, coords, counts, rows_n, parts):
    maxt, tile, _ = tiles.shape
    fw, nodes = features.shape
    outs = weight_t.shape[1]
    width = outs // parts
    feat = fw * rows_n
    block = nodes // rows_n
    rows = nodes * parts // rows_n
    trow = rows // tile
    bunches = maxt // BUNCH + trow * (BUNCH - 1) // BUNCH
    spots = -(-bunches * BUNCH // 128) * 128
    chunks = outs // HALF
    split = width // HALF
    kind = features.dtype
    smem = pl.BlockSpec(memory_space=pltpu.SMEM)
    vmem = pl.BlockSpec(memory_space=pltpu.VMEM)
    dma = pltpu.SemaphoreType.DMA
    return pl.pallas_call(
        functools.partial(layer_kernel, rows_n, parts),
        out_shape=jax.ShapeDtypeStruct((rows, width), kind),
        in_specs=[smem, vmem, vmem, vmem, pl.BlockSpec(memory_space=pl.ANY)],
        out_specs=vmem,
        scratch_shapes=[
            pltpu.VMEM((maxt + 1, tile, tile), kind),
            pltpu.VMEM((feat, block), kind),
            pltpu.VMEM((block, feat), kind),
            pltpu.VMEM((parts, fw, width), kind),
            [pltpu.VMEM((feat, width), kind) for _ in range(parts)],
            [pltpu.VMEM((nodes // tile // 2, tile, tile), kind) for _ in range(chunks)],
            pltpu.VMEM((nodes // tile, tile, tile), kind),
            pltpu.VMEM((bunches + 1, tile, tile), kind),
            pltpu.VMEM((chunks, rows // 2, tile), kind),
            pltpu.VMEM((chunks + split, rows // 2, tile), kind),
            pltpu.VMEM((8, spots), jnp.int32),
            pltpu.VMEM((8, spots), jnp.float32),
            pltpu.SMEM((8, spots), jnp.int32),
            pltpu.SMEM((8, spots), jnp.float32),
            dma((3,)),
            dma((rows_n,)),
            dma((rows_n,)),
            dma((parts, rows_n)),
            dma((parts, rows_n)),
            dma((chunks, rows_n)),
            dma((chunks, rows_n)),
            dma((chunks, rows_n)),
            dma((chunks, PIECES)),
            dma((chunks + split, PIECES)),
        ],
        compiler_params=pltpu.CompilerParams(
            collective_id=0, has_side_effects=True, vmem_limit_bytes=VMEM_LIMIT
        ),
        name="layer",
    )(counts, coords, features, weight_t, tiles)


def solution(mesh):
    placed = (
        P("col", "row"),
        P(None, "row"),
        P(("row", "col"), None, None),
        P(None, ("row", "col")),
        P(("row", "col")),
    )
    rows_n = mesh.shape["row"]
    parts = mesh.shape["col"]

    def body(features, weight_t, tiles, coords, counts):
        return layer(features.T, weight_t.T, tiles, coords, counts, rows_n, parts)

    return jax.shard_map(
        body, mesh=mesh, in_specs=placed, out_specs=P("row", "col"), check_vma=False
    )
```

time: 151 us -> 119 us (0.79); the launches traced: 149 us -> 119 us
  Pallas kernels: 146 us -> 116 us
    pallas_call x1, Pallas kernels: 142 us -> 116 us  [layer(): pl.pallas_call(functools.partial(layer_kernel, rows_n, parts), out_shape=...]
    pallas_call x1 -> x0, Pallas kernels: 4.34 us -> none  [plan(): pl.pallas_call(plan_kernel, out_shape=[jax.ShapeDtypeStruct((bunches * BU...]
where the time goes in v2:
time: 119 us
  Pallas kernels  116 us (97%)
  local copies, waits for them, and re-layouts  2.26 us (2%)
    pallas_call x1, Pallas kernels, layer(): pl.pallas_call(functools.partial(layer_kernel, rows_n, parts), out_shape=...  116 us

profile of v2, /device:TPU:16, one launch (start us, length us, event | category | flops | bytes accessed | tf_op | source)
XLA Modules:
  0.0 119.0 jit_solution(7217164025911254792)
XLA Ops:
  0.7 116.0 %layer.1 = bf16[4096,128]{1,0:T(8,128)(2,1)} custom-call(s32[1]{0:T(128)S(6)} %copy.7.count_ref, s32[2,256]{1,0:T(2,128)} %coords_ref.1, bf16[64,8192]{1,0:T(8,128)(2,1)} %bitcast.2, bf16[64,512]{1,0:T(8,128)(2,1)} %bitcast.3, bf16[256,128,128]{2,1,0:T(8,128)(2,1)} %tiles_hbm.1), custom_call_target="tpu_custom_call" | custom-call | tf_op jit(solution)/shard_map/layer/pallas_call | solution.py:308
  116.7 2.3 %copy.8 = bf16[4096,128]{1,0:T(8,128)(2,1)} copy(bf16[4096,128]{1,0:T(8,128)(2,1)} %layer.1) | data formatting | bytes 2097152

commit v3 on v2

--- a/solution.py
+++ b/solution.py
@@ -8,9 +8,8 @@
 from jax.sharding import PartitionSpec as P
 
 BUNCH = 2
-UNROLL = 16
+UNROLL = 36
 PIECES = 4
-EARLY = 2
 HALF = 64
 VMEM_LIMIT = 62 * 1024 * 1024
 
@@ -78,7 +77,8 @@
     maxt, tile, _ = tiles_hbm.shape
     fw, nodes = f_ref.shape
     block = nodes // rows_n
-    deep = block // tile // 2
+    half = block // 2
+    deep = block // tile // 4
     rows, width = out_ref.shape
     split = width // HALF
     chunks = parts * split
@@ -110,12 +110,12 @@
 
     low_half = here < parts - 1 - here
     few = jnp.minimum(here, parts - 1 - here)
-    order = []
-    for k in range(parts - 1):
-        step = jnp.where(k < 2 * few, k // 2, k - few)
-        first = jnp.where(k < 2 * few, k % 2, 0) == 0
-        order.append(jnp.where(first == low_half, parts - 1 - step, step))
-    order.append(here)
+
+    def target(k):
+        paired = k < 2 * few
+        step = jnp.where(paired, k // 2, k - few)
+        first = jnp.where(paired, k % 2, 0) == 0
+        return jnp.where(k == parts - 1, here, jnp.where(first == low_half, parts - 1 - step, step))
 
     for q in range(parts):
         w_mine[q] = w_ref[:, q * width:(q + 1) * width]
@@ -128,22 +128,22 @@
 
     def send_weight(k):
         for step in range(1, rows_n):
-            begin(remote(w_mine.at[order[k]], weights[k].at[pl.ds(pl.multiple_of(me * fw, fw), fw)],
+            begin(remote(w_mine.at[target(k)], weights[k].at[pl.ds(pl.multiple_of(me * fw, fw), fw)],
                          w_send.at[k, step], w_recv.at[k, me], "row", lax.rem(me + step, rows_n)))
 
     send_weight(0)
-    for step in range(1, rows_n):
-        to = lax.rem(me + step, rows_n)
-        begin(remote(f_ref.at[:, pl.ds(pl.multiple_of(to * block, block), block)],
-                     ft.at[pl.ds(pl.multiple_of(me * fw, fw), fw)],
-                     f_send.at[step], f_recv.at[me], "row", to))
-    for k in range(1, EARLY):
-        send_weight(k)
+    for part in range(2):
+        for step in range(1, rows_n):
+            to = lax.rem(me + step, rows_n)
+            begin(remote(f_ref.at[:, pl.ds(pl.multiple_of(to * block + part * half, half), half)],
+                         ft.at[part, pl.ds(pl.multiple_of(me * fw, fw), fw)],
+                         f_send.at[part, step], f_recv.at[part, me], "row", to))
 
     mine = pl.ds(pl.multiple_of(me * fw, fw), fw)
-    ft[mine, :] = f_ref[:, pl.ds(pl.multiple_of(me * block, block), block)]
+    for part in range(2):
+        ft[part, mine, :] = f_ref[:, pl.ds(pl.multiple_of(me * block + part * half, half), half)]
     for k in range(parts):
-        weights[k][mine, :] = w_mine[order[k]]
+        weights[k][mine, :] = w_mine[target(k)]
 
     tiles_ref[maxt] = jnp.zeros((tile, tile), tiles_ref.dtype)
     runs[bunches] = jnp.zeros((tile, tile), runs.dtype)
@@ -161,52 +161,65 @@
             place = weights[k].at[pl.ds(pl.multiple_of(at * fw, fw), fw)]
             remote(place, place, w_send.at[k, step], w_recv.at[k, at], "row", at).wait_recv()
 
-    for step in range(1, rows_n):
-        at = lax.rem(me + step, rows_n)
-        place = ft.at[pl.ds(pl.multiple_of(at * fw, fw), fw)]
-        remote(place, place, f_send.at[step], f_recv.at[at], "row", at).wait_recv()
-    strip = min(block, 512)
-    for low in range(0, feat, tile):
-        for at in range(0, block, strip):
-            xs[at:at + strip, low:low + tile] = ft[low:low + tile, at:at + strip].T
-
-    def spot(c, at):
-        return panels[c].at[pl.ds(at * deep, deep)]
-
-    def share(k):
-        weight_in(k)
-        product = jnp.dot(xs[...], weights[k][...], preferred_element_type=jnp.float32).astype(xs.dtype)
+    group = tile // fw
+    groups = rows_n // group
+    strip = min(half, 512)
+
+    def turn_in(part):
+        for turn in range(groups):
+            low = lax.rem(me // group + turn, groups) * group
+            for j in range(group):
+                at = low + j
+                place = ft.at[part, pl.ds(pl.multiple_of(at * fw, fw), fw)]
+
+                @pl.when(at != me)
+                def _():
+                    remote(place, place, f_send.at[part, 0], f_recv.at[part, at], "row", me).wait_recv()
+
+            lane = pl.ds(pl.multiple_of(low * fw, tile), tile)
+            for at in range(0, half, strip):
+                xs[part * half + at:part * half + at + strip, lane] = ft[part, lane, at:at + strip].T
+
+    def spot(c, at, part):
+        if part is None:
+            return panels.at[c, pl.ds(at * 2 * deep, 2 * deep)]
+        return panels.at[c, pl.ds((at * 2 + part) * deep, deep)]
+
+    def row_of(c, part):
+        return chunks if part == 1 else c
+
+    def send_chunk(c, part):
+        place, line = spot(c, me, part), row_of(c, part)
+        for step in range(1, twins):
+            begin(remote(place, place, h_send.at[line, step], h_recv.at[line, me], "row",
+                         lax.rem(me + 2 * step, rows_n)))
+        begin(remote(place, place, h_send.at[line, 0], h_recv.at[line, me], "row", sibling))
+
+    def make(k, part):
+        product = jnp.dot(xs[part * half:(part + 1) * half, :], weights[k][...],
+                          preferred_element_type=jnp.float32).astype(xs.dtype)
         for h in range(split):
-            c = k * split + h
             cut = product[:, h * HALF:(h + 1) * HALF]
-            packed = jnp.concatenate([cut[:block // 2], cut[block // 2:]], axis=1)
-            panels[c][pl.ds(me * deep, deep)] = packed.reshape(deep, tile, tile)
+            packed = jnp.concatenate([cut[:half // 2], cut[half // 2:]], axis=1)
+            panels[k * split + h, pl.ds((me * 2 + part) * deep, deep)] = packed.reshape(deep, tile, tile)
+
+    def forward(c, at, step, part):
+        place, line = spot(c, at, part), row_of(c, part)
+        return remote(place, place, sib_send.at[line, step], h_recv.at[line, at], "row", sibling)
+
+    def collect(c, sections):
+        for part in sections:
             for step in range(1, twins):
-                begin(remote(spot(c, me), spot(c, me), h_send.at[c, step], h_recv.at[c, me], "row",
-                             lax.rem(me + 2 * step, rows_n)))
-            begin(remote(spot(c, me), spot(c, me), h_send.at[c, 0], h_recv.at[c, me], "row", sibling))
-
-    for k in range(EARLY):
-        share(k)
-    for k in range(EARLY, parts):
-        send_weight(k)
-    fetch.wait()
-    for move in moves:
-        move.wait()
-
-    def collect(c):
-        for step in range(1, twins):
-            at = lax.rem(me + 2 * step, rows_n)
-            passed = remote(spot(c, at), spot(c, at), sib_send.at[c, step], h_recv.at[c, at], "row", sibling)
-            passed.wait_recv()
-            begin(passed)
-        for step in range(twins):
-            at = lax.rem(sibling + 2 * step, rows_n)
-            remote(spot(c, at), spot(c, at), sib_send.at[c, step], h_recv.at[c, at], "row", sibling).wait_recv()
+                passed = forward(c, lax.rem(me + 2 * step, rows_n), step, part)
+                passed.wait_recv()
+                passed.start()
+        for part in sections:
+            for step in range(twins):
+                forward(c, lax.rem(sibling + 2 * step, rows_n), step, part).wait_recv()
 
     def multiply(c):
-        for at in range(rows_n * deep):
-            both = panels[c][at]
+        for at in range(rows_n * 2 * deep):
+            both = panels[c, at]
             low = at // deep * 2 * deep + at % deep
             spread[low] = both
             spread[low + deep] = jnp.concatenate([both[:, HALF:], both[:, :HALF]], axis=1)
@@ -234,37 +247,60 @@
     def piece(ref, which, p):
         return ref.at[which, pl.ds(p * thick, thick)]
 
+    def outgoing(c, p):
+        q = target(c // split)
+        to = jnp.where(q > here, here + 1, here - 1)
+        goes = jnp.where(q == here - 1, parts, q) * split + c % split
+        return remote(piece(partial, c, p), piece(landed, goes, p), z_send.at[c, p], z_recv.at[goes, p],
+                      "col", to)
+
     def stream(c):
-        q = order[c // split]
-        up = q > here
-        inner = (here > 0) & (here < parts - 1)
-        to = jnp.where(up, here + 1, here - 1)
-        came = q * split + c % split
-        goes = jnp.where(q == here - 1, parts, q) * split + c % split
+        came = target(c // split) * split + c % split
         for p in range(PIECES):
-            span = slice(p * thick, (p + 1) * thick)
-
-            @pl.when(inner)
+            @pl.when((here > 0) & (here < parts - 1))
             def _():
-                remote(piece(landed, came, p), piece(landed, came, p), z_send.at[c, p], z_recv.at[came, p],
-                       "col", to).wait_recv()
+                span = slice(p * thick, (p + 1) * thick)
+                place = piece(landed, came, p)
+                remote(place, place, z_send.at[c, p], z_recv.at[came, p], "col", here).wait_recv()
                 partial[c, span, :] = (partial[c, span, :].astype(jnp.float32)
                                        + landed[came, span, :].astype(jnp.float32)).astype(partial.dtype)
 
-            begin(remote(piece(partial, c, p), piece(landed, goes, p), z_send.at[c, p], z_recv.at[goes, p],
-                         "col", to))
-
-    for c in range(chunks - split):
-        collect(c)
+            outgoing(c, p).start()
+
+    for part in range(2):
+        turn_in(part)
+        if part == 0:
+            weight_in(0)
+        make(0, part)
+        send_chunk(0, part)
+    for h in range(1, split):
+        send_chunk(h, None)
+    for k in range(1, parts):
+        send_weight(k)
+    fetch.wait()
+    for move in moves:
+        move.wait()
+    collect(0, (0, 1))
+    multiply(0)
+    stream(0)
+    for k in range(1, parts):
+        weight_in(k)
+        for part in range(2):
+            make(k, part)
+        for h in range(split):
+            send_chunk(k * split + h, None)
+
+    def phase(c, carry):
+        collect(c, (None,))
         multiply(c)
-        stream(c)
-        if c == 0:
-            for later in range(EARLY, parts):
-                share(later)
-    for h in range(split):
-        c = chunks - split + h
-        collect(c)
-        multiply(c)
+
+        @pl.when(c < chunks - split)
+        def _():
+            stream(c)
+
+        return carry
+
+    lax.fori_loop(1, chunks, phase, 0)
     for p in range(PIECES):
         for h in range(split):
             span = slice(p * thick, (p + 1) * thick)
@@ -286,6 +322,23 @@
             out_ref[high, h * HALF:(h + 1) * HALF] = total[:, HALF:]
     for copy in issued:
         copy.wait_send()
+    for part in range(2):
+        for step in range(1, twins):
+            forward(0, lax.rem(me + 2 * step, rows_n), step, part).wait_send()
+
+    def settle(c, carry):
+        for step in range(1, twins):
+            forward(c, lax.rem(me + 2 * step, rows_n), step, None).wait_send()
+        return carry
+
+    lax.fori_loop(1, chunks, settle, 0)
+
+    def drain(c, carry):
+        for p in range(PIECES):
+            outgoing(c, p).wait_send()
+        return carry
+
+    lax.fori_loop(0, chunks - split, drain, 0)
 
 
 def layer(features, weight_t, tiles, coords, counts, rows_n, parts):
@@ -312,11 +365,11 @@
         out_specs=vmem,
         scratch_shapes=[
             pltpu.VMEM((maxt + 1, tile, tile), kind),
-            pltpu.VMEM((feat, block), kind),
+            pltpu.VMEM((2, feat, block // 2), kind),
             pltpu.VMEM((block, feat), kind),
             pltpu.VMEM((parts, fw, width), kind),
             [pltpu.VMEM((feat, width), kind) for _ in range(parts)],
-            [pltpu.VMEM((nodes // tile // 2, tile, tile), kind) for _ in range(chunks)],
+            pltpu.VMEM((chunks, nodes // tile // 2, tile, tile), kind),
             pltpu.VMEM((nodes // tile, tile, tile), kind),
             pltpu.VMEM((bunches + 1, tile, tile), kind),
             pltpu.VMEM((chunks, rows // 2, tile), kind),
@@ -326,13 +379,13 @@
             pltpu.SMEM((8, spots), jnp.int32),
             pltpu.SMEM((8, spots), jnp.float32),
             dma((3,)),
-            dma((rows_n,)),
-            dma((rows_n,)),
+            dma((2, rows_n)),
+            dma((2, rows_n)),
             dma((parts, rows_n)),
             dma((parts, rows_n)),
-            dma((chunks, rows_n)),
-            dma((chunks, rows_n)),
-            dma((chunks, rows_n)),
+            dma((chunks + 1, rows_n)),
+            dma((chunks + 1, rows_n)),
+            dma((chunks + 1, rows_n)),
             dma((chunks, PIECES)),
             dma((chunks + split, PIECES)),
         ],

time: 119 us -> 107 us (0.90)
  Pallas kernels: 116 us -> 104 us
    pallas_call x1, Pallas kernels: 116 us -> 104 us  [layer(): pl.pallas_call(functools.partial(layer_kernel, rows_n, parts), out_shape=...]
where the time goes in v3:
time: 107 us
  Pallas kernels  104 us (97%)
  local copies, waits for them, and re-layouts  2.26 us (2%)
    pallas_call x1, Pallas kernels, layer(): pl.pallas_call(functools.partial(layer_kernel, rows_n, parts), out_shape=...  104 us
    unnamed x1, local copies, waits for them, and re-layouts  2.26 us

profile of v3, /device:TPU:16, one launch (start us, length us, event | category | flops | bytes accessed | tf_op | source)
XLA Modules:
  0.0 106.6 jit_solution(15412568651856159919)
XLA Ops:
  0.7 103.7 %layer.1 = bf16[4096,128]{1,0:T(8,128)(2,1)} custom-call(s32[1]{0:T(128)S(6)} %copy.7.count_ref, s32[2,256]{1,0:T(2,128)} %coords_ref.1, bf16[64,8192]{1,0:T(8,128)(2,1)} %bitcast.2, bf16[64,512]{1,0:T(8,128)(2,1)} %bitcast.3, bf16[256,128,128]{2,1,0:T(8,128)(2,1)} %tiles_hbm.1), custom_call_target="tpu_custom_call" | custom-call | tf_op jit(solution)/shard_map/layer/pallas_call | solution.py:361
  104.4 2.3 %copy.8 = bf16[4096,128]{1,0:T(8,128)(2,1)} copy(bf16[4096,128]{1,0:T(8,128)(2,1)} %layer.1) | data formatting | bytes 2097152

commit v4 on v3

--- a/solution.py
+++ b/solution.py
@@ -9,6 +9,7 @@
 
 BUNCH = 2
 UNROLL = 36
+CUTS = 2
 PIECES = 4
 HALF = 64
 VMEM_LIMIT = 62 * 1024 * 1024
@@ -68,8 +69,8 @@
     lists_ref[2:3, 0:128] = jnp.where(slot[:, :128] < trow, last, 0)
 
 
-def layer_kernel(rows_n, parts, count_ref, coords_ref, f_ref, w_ref, tiles_hbm, out_ref,
-                 tiles_ref, ft, xs, w_mine, weights, panels, spread, runs, partial, landed,
+def layer_kernel(rows_n, parts, count_hbm, coords_hbm, f_hbm, w_hbm, tiles_hbm, out_ref,
+                 count_ref, coords_ref, f_ref, w_ref, tiles_ref, ft, xs, w_mine, weights, panels, spread, runs, partial, landed,
                  lists_made, keep_made, lists_ref, keep_ref,
                  local_sem, f_send, f_recv, w_send, w_recv, h_send, h_recv, sib_send, z_send, z_recv):
     me = lax.axis_index("row")
@@ -77,8 +78,11 @@
     maxt, tile, _ = tiles_hbm.shape
     fw, nodes = f_ref.shape
     block = nodes // rows_n
-    half = block // 2
-    deep = block // tile // 4
+    cuts = ft.shape[0]
+    cut = block // cuts
+    deep = cut // tile // 2
+    whole = block // tile // 2
+    group = tile // fw
     rows, width = out_ref.shape
     split = width // HALF
     chunks = parts * split
@@ -89,8 +93,14 @@
     sibling = me + 1 - 2 * core
     twins = rows_n // 2
 
-    fetch = pltpu.make_async_copy(tiles_hbm, tiles_ref.at[pl.ds(0, maxt)], local_sem.at[0])
-    fetch.start()
+    loads = [
+        pltpu.make_async_copy(source, dest, local_sem.at[at]) for at, (source, dest) in enumerate((
+            (f_hbm, f_ref), (w_hbm, w_ref), (coords_hbm, coords_ref), (count_hbm, count_ref),
+            (tiles_hbm, tiles_ref.at[pl.ds(0, maxt)])))
+    ]
+    for load in loads:
+        load.start()
+    fetch = loads.pop()
 
     barrier = pltpu.get_barrier_semaphore()
     for step in range(1, rows_n):
@@ -117,31 +127,27 @@
         first = jnp.where(paired, k % 2, 0) == 0
         return jnp.where(k == parts - 1, here, jnp.where(first == low_half, parts - 1 - step, step))
 
+    for load in loads:
+        load.wait()
     for q in range(parts):
         w_mine[q] = w_ref[:, q * width:(q + 1) * width]
 
-    issued = []
-
-    def begin(copy):
-        copy.start()
-        issued.append(copy)
-
     def send_weight(k):
         for step in range(1, rows_n):
-            begin(remote(w_mine.at[target(k)], weights[k].at[pl.ds(pl.multiple_of(me * fw, fw), fw)],
-                         w_send.at[k, step], w_recv.at[k, me], "row", lax.rem(me + step, rows_n)))
+            remote(w_mine.at[target(k)], weights[k].at[pl.ds(pl.multiple_of(me * fw, fw), fw)],
+                   w_send.at[k], w_recv.at[k], "row", lax.rem(me + step, rows_n)).start()
 
     send_weight(0)
-    for part in range(2):
+    for part in range(cuts):
         for step in range(1, rows_n):
             to = lax.rem(me + step, rows_n)
-            begin(remote(f_ref.at[:, pl.ds(pl.multiple_of(to * block + part * half, half), half)],
-                         ft.at[part, pl.ds(pl.multiple_of(me * fw, fw), fw)],
-                         f_send.at[part, step], f_recv.at[part, me], "row", to))
+            remote(f_ref.at[:, pl.ds(pl.multiple_of(to * block + part * cut, cut), cut)],
+                   ft.at[part, pl.ds(pl.multiple_of(me * fw, fw), fw)],
+                   f_send.at[0], f_recv.at[part, me // group], "row", to).start()
 
     mine = pl.ds(pl.multiple_of(me * fw, fw), fw)
-    for part in range(2):
-        ft[part, mine, :] = f_ref[:, pl.ds(pl.multiple_of(me * block + part * half, half), half)]
+    for part in range(cuts):
+        ft[part, mine, :] = f_ref[:, pl.ds(pl.multiple_of(me * block + part * cut, cut), cut)]
     for k in range(parts):
         weights[k][mine, :] = w_mine[target(k)]
 
@@ -149,76 +155,70 @@
     runs[bunches] = jnp.zeros((tile, tile), runs.dtype)
     plan(coords_ref, count_ref[0], trow, lists_made, keep_made)
     moves = [
-        pltpu.make_async_copy(lists_made, lists_ref, local_sem.at[1]),
-        pltpu.make_async_copy(keep_made, keep_ref, local_sem.at[2]),
+        pltpu.make_async_copy(lists_made, lists_ref, local_sem.at[5]),
+        pltpu.make_async_copy(keep_made, keep_ref, local_sem.at[6]),
     ]
     for move in moves:
         move.start()
 
-    def weight_in(k):
-        for step in range(1, rows_n):
-            at = lax.rem(me + step, rows_n)
-            place = weights[k].at[pl.ds(pl.multiple_of(at * fw, fw), fw)]
-            remote(place, place, w_send.at[k, step], w_recv.at[k, at], "row", at).wait_recv()
-
-    group = tile // fw
+    def others(ref, number):
+        return ref.at[pl.ds(0, number)]
+
+    def weight_of(k):
+        place = others(weights[k], (rows_n - 1) * fw)
+        return remote(place, place, w_send.at[k], w_recv.at[k], "row", sibling)
+
     groups = rows_n // group
-    strip = min(half, 512)
+    strip = min(cut, 512)
 
     def turn_in(part):
         for turn in range(groups):
-            low = lax.rem(me // group + turn, groups) * group
-            for j in range(group):
-                at = low + j
-                place = ft.at[part, pl.ds(pl.multiple_of(at * fw, fw), fw)]
-
-                @pl.when(at != me)
-                def _():
-                    remote(place, place, f_send.at[part, 0], f_recv.at[part, at], "row", me).wait_recv()
-
-            lane = pl.ds(pl.multiple_of(low * fw, tile), tile)
-            for at in range(0, half, strip):
-                xs[part * half + at:part * half + at + strip, lane] = ft[part, lane, at:at + strip].T
+            at = lax.rem(me // group + turn, groups)
+            due = (group if turn else group - 1) * fw
+            if due:
+                place = others(ft.at[part], due)
+                remote(place, place, f_send.at[0], f_recv.at[part, at], "row", sibling).wait_recv()
+            lane = pl.ds(pl.multiple_of(at * tile, tile), tile)
+            for low in range(0, cut, strip):
+                xs[part * cut + low:part * cut + low + strip, lane] = ft[part, lane, low:low + strip].T
 
     def spot(c, at, part):
         if part is None:
-            return panels.at[c, pl.ds(at * 2 * deep, 2 * deep)]
-        return panels.at[c, pl.ds((at * 2 + part) * deep, deep)]
-
-    def row_of(c, part):
-        return chunks if part == 1 else c
+            return panels.at[c, pl.ds(at * whole, whole)]
+        return panels.at[c, pl.ds(at * whole + part * deep, deep)]
+
+    def line_of(c, part):
+        return chunks + part - 1 if part else c
 
     def send_chunk(c, part):
-        place, line = spot(c, me, part), row_of(c, part)
+        place, line = spot(c, me, part), line_of(c, part)
         for step in range(1, twins):
-            begin(remote(place, place, h_send.at[line, step], h_recv.at[line, me], "row",
-                         lax.rem(me + 2 * step, rows_n)))
-        begin(remote(place, place, h_send.at[line, 0], h_recv.at[line, me], "row", sibling))
+            remote(place, place, h_send.at[0], h_recv.at[line, 0], "row", lax.rem(me + 2 * step, rows_n)).start()
+        remote(place, place, h_send.at[0], h_recv.at[line, 1], "row", sibling).start()
+
+    def awaited(c, part, number, way):
+        place = others(panels.at[c], number * (whole if part is None else deep))
+        remote(place, place, h_send.at[0], h_recv.at[line_of(c, part), way], "row", sibling).wait_recv()
 
     def make(k, part):
-        product = jnp.dot(xs[part * half:(part + 1) * half, :], weights[k][...],
+        product = jnp.dot(xs[part * cut:(part + 1) * cut, :], weights[k][...],
                           preferred_element_type=jnp.float32).astype(xs.dtype)
         for h in range(split):
-            cut = product[:, h * HALF:(h + 1) * HALF]
-            packed = jnp.concatenate([cut[:half // 2], cut[half // 2:]], axis=1)
-            panels[k * split + h, pl.ds((me * 2 + part) * deep, deep)] = packed.reshape(deep, tile, tile)
-
-    def forward(c, at, step, part):
-        place, line = spot(c, at, part), row_of(c, part)
-        return remote(place, place, sib_send.at[line, step], h_recv.at[line, at], "row", sibling)
+            band = product[:, h * HALF:(h + 1) * HALF]
+            packed = jnp.concatenate([band[:cut // 2], band[cut // 2:]], axis=1)
+            panels[k * split + h, pl.ds(me * whole + part * deep, deep)] = packed.reshape(deep, tile, tile)
 
     def collect(c, sections):
         for part in sections:
+            awaited(c, part, twins - 1, 0)
             for step in range(1, twins):
-                passed = forward(c, lax.rem(me + 2 * step, rows_n), step, part)
-                passed.wait_recv()
-                passed.start()
+                place = spot(c, lax.rem(me + 2 * step, rows_n), part)
+                remote(place, place, sib_send.at[0], h_recv.at[line_of(c, part), 1], "row", sibling).start()
         for part in sections:
-            for step in range(twins):
-                forward(c, lax.rem(sibling + 2 * step, rows_n), step, part).wait_recv()
+            awaited(c, part, twins, 1)
 
     def multiply(c):
-        for at in range(rows_n * 2 * deep):
+        for at in range(rows_n * whole):
             both = panels[c, at]
             low = at // deep * 2 * deep + at % deep
             spread[low] = both
@@ -251,7 +251,7 @@
         q = target(c // split)
         to = jnp.where(q > here, here + 1, here - 1)
         goes = jnp.where(q == here - 1, parts, q) * split + c % split
-        return remote(piece(partial, c, p), piece(landed, goes, p), z_send.at[c, p], z_recv.at[goes, p],
+        return remote(piece(partial, c, p), piece(landed, goes, p), z_send.at[0], z_recv.at[goes, p],
                       "col", to)
 
     def stream(c):
@@ -261,16 +261,16 @@
             def _():
                 span = slice(p * thick, (p + 1) * thick)
                 place = piece(landed, came, p)
-                remote(place, place, z_send.at[c, p], z_recv.at[came, p], "col", here).wait_recv()
+                remote(place, place, z_send.at[0], z_recv.at[came, p], "col", here).wait_recv()
                 partial[c, span, :] = (partial[c, span, :].astype(jnp.float32)
                                        + landed[came, span, :].astype(jnp.float32)).astype(partial.dtype)
 
             outgoing(c, p).start()
 
-    for part in range(2):
+    for part in range(cuts):
         turn_in(part)
         if part == 0:
-            weight_in(0)
+            weight_of(0).wait_recv()
         make(0, part)
         send_chunk(0, part)
     for h in range(1, split):
@@ -280,12 +280,12 @@
     fetch.wait()
     for move in moves:
         move.wait()
-    collect(0, (0, 1))
+    collect(0, tuple(range(cuts)))
     multiply(0)
     stream(0)
     for k in range(1, parts):
-        weight_in(k)
-        for part in range(2):
+        weight_of(k).wait_recv()
+        for part in range(cuts):
             make(k, part)
         for h in range(split):
             send_chunk(k * split + h, None)
@@ -310,7 +310,7 @@
             for slot, there in ((below, here > 0), (above, here < parts - 1)):
                 @pl.when(there)
                 def _():
-                    remote(piece(landed, slot, p), piece(landed, slot, p), z_send.at[c, p], z_recv.at[slot, p],
+                    remote(piece(landed, slot, p), piece(landed, slot, p), z_send.at[0], z_recv.at[slot, p],
                            "col", here).wait_recv()
 
             total = partial[c, span, :].astype(jnp.float32)
@@ -320,25 +320,16 @@
             high = slice(rows // 2 + p * thick, rows // 2 + (p + 1) * thick)
             out_ref[span, h * HALF:(h + 1) * HALF] = total[:, :HALF]
             out_ref[high, h * HALF:(h + 1) * HALF] = total[:, HALF:]
-    for copy in issued:
-        copy.wait_send()
-    for part in range(2):
-        for step in range(1, twins):
-            forward(0, lax.rem(me + 2 * step, rows_n), step, part).wait_send()
-
-    def settle(c, carry):
-        for step in range(1, twins):
-            forward(c, lax.rem(me + 2 * step, rows_n), step, None).wait_send()
-        return carry
-
-    lax.fori_loop(1, chunks, settle, 0)
-
-    def drain(c, carry):
-        for p in range(PIECES):
-            outgoing(c, p).wait_send()
-        return carry
-
-    lax.fori_loop(0, chunks - split, drain, 0)
+    for k in range(parts):
+        weight_of(k).wait_send()
+    place = ft.at[:, pl.ds(0, (rows_n - 1) * fw)]
+    remote(place, place, f_send.at[0], f_recv.at[0, 0], "row", sibling).wait_send()
+    place = panels.at[:, pl.ds(0, twins * whole)]
+    remote(place, place, h_send.at[0], h_recv.at[0, 0], "row", sibling).wait_send()
+    place = panels.at[:, pl.ds(0, (twins - 1) * whole)]
+    remote(place, place, sib_send.at[0], h_recv.at[0, 0], "row", sibling).wait_send()
+    place = partial.at[pl.ds(0, chunks - split)]
+    remote(place, place, z_send.at[0], z_recv.at[0, 0], "col", here).wait_send()
 
 
 def layer(features, weight_t, tiles, coords, counts, rows_n, parts):
@@ -354,18 +345,22 @@
     spots = -(-bunches * BUNCH // 128) * 128
     chunks = outs // HALF
     split = width // HALF
+    cuts = min(CUTS, block // (2 * tile))
     kind = features.dtype
-    smem = pl.BlockSpec(memory_space=pltpu.SMEM)
     vmem = pl.BlockSpec(memory_space=pltpu.VMEM)
     dma = pltpu.SemaphoreType.DMA
     return pl.pallas_call(
         functools.partial(layer_kernel, rows_n, parts),
         out_shape=jax.ShapeDtypeStruct((rows, width), kind),
-        in_specs=[smem, vmem, vmem, vmem, pl.BlockSpec(memory_space=pl.ANY)],
+        in_specs=[pl.BlockSpec(memory_space=pltpu.HBM)] * 5,
         out_specs=vmem,
         scratch_shapes=[
+            pltpu.SMEM(counts.shape, jnp.int32),
+            pltpu.VMEM(coords.shape, jnp.int32),
+            pltpu.VMEM(features.shape, kind),
+            pltpu.VMEM(weight_t.shape, kind),
             pltpu.VMEM((maxt + 1, tile, tile), kind),
-            pltpu.VMEM((2, feat, block // 2), kind),
+            pltpu.VMEM((cuts, feat, block // cuts), kind),
             pltpu.VMEM((block, feat), kind),
             pltpu.VMEM((parts, fw, width), kind),
             [pltpu.VMEM((feat, width), kind) for _ in range(parts)],
@@ -378,15 +373,15 @@
             pltpu.VMEM((8, spots), jnp.float32),
             pltpu.SMEM((8, spots), jnp.int32),
             pltpu.SMEM((8, spots), jnp.float32),
-            dma((3,)),
-            dma((2, rows_n)),
-            dma((2, rows_n)),
-            dma((parts, rows_n)),
-            dma((parts, rows_n)),
-            dma((chunks + 1, rows_n)),
-            dma((chunks + 1, rows_n)),
-            dma((chunks + 1, rows_n)),
-            dma((chunks, PIECES)),
+            dma((7,)),
+            dma((1,)),
+            dma((cuts, feat // tile)),
+            dma((parts,)),
+            dma((parts,)),
+            dma((1,)),
+            dma((chunks + cuts - 1, 2)),
+            dma((1,)),
+            dma((1,)),
             dma((chunks + split, PIECES)),
         ],
         compiler_params=pltpu.CompilerParams(

time: 107 us -> 103 us (0.963)
  Pallas kernels: 104 us -> 99.6 us
    pallas_call x1, Pallas kernels: 104 us -> 99.6 us  [layer(): pl.pallas_call(functools.partial(layer_kernel, rows_n, parts), out_shape=...]
where the time goes in v4:
time: 103 us
  Pallas kernels  99.6 us (97%)
  local copies, waits for them, and re-layouts  2.26 us (2%)
    pallas_call x1, Pallas kernels, layer(): pl.pallas_call(functools.partial(layer_kernel, rows_n, parts), out_shape=...  99.6 us
    unnamed x1, local copies, waits for them, and re-layouts  2.26 us

profile of v4, /device:TPU:16, one launch (start us, length us, event | category | flops | bytes accessed | tf_op | source)
XLA Modules:
  0.0 102.5 jit_solution(7341796716401795366)
XLA Ops:
  0.7 99.6 %layer.1 = bf16[4096,128]{1,0:T(8,128)(2,1)} custom-call(s32[1]{0:T(128)S(6)} %copy.7.count_hbm, s32[2,256]{1,0:T(2,128)} %coords_hbm.1, bf16[64,8192]{1,0:T(8,128)(2,1)} %bitcast.2, bf16[64,512]{1,0:T(8,128)(2,1)} %bitcast.3, bf16[256,128,128]{2,1,0:T(8,128)(2,1)} %tiles_hbm.1), custom_call_target="tpu_custom_call" | custom-call | tf_op jit(solution)/shard_map/layer/pallas_call | solution.py:352
  100.2 2.3 %copy.8 = bf16[4096,128]{1,0:T(8,128)(2,1)} copy(bf16[4096,128]{1,0:T(8,128)(2,1)} %layer.1) | data formatting | bytes 2097152

commit v5 on v4

--- a/solution.py
+++ b/solution.py
@@ -132,12 +132,16 @@
     for q in range(parts):
         w_mine[q] = w_ref[:, q * width:(q + 1) * width]
 
+    alike = [lax.rem(me + 2 * step, rows_n) for step in range(1, twins)]
+
     def send_weight(k):
         for step in range(1, rows_n):
             remote(w_mine.at[target(k)], weights[k].at[pl.ds(pl.multiple_of(me * fw, fw), fw)],
                    w_send.at[k], w_recv.at[k], "row", lax.rem(me + step, rows_n)).start()
 
-    send_weight(0)
+    for to, way in [(twin, 0) for twin in alike] + [(sibling, parts)]:
+        remote(w_mine.at[target(0)], weights[0].at[pl.ds(pl.multiple_of(me * fw, fw), fw)],
+               w_send.at[0], w_recv.at[way], "row", to).start()
     for part in range(cuts):
         for step in range(1, rows_n):
             to = lax.rem(me + step, rows_n)
@@ -164,9 +168,15 @@
     def others(ref, number):
         return ref.at[pl.ds(0, number)]
 
-    def weight_of(k):
-        place = others(weights[k], (rows_n - 1) * fw)
-        return remote(place, place, w_send.at[k], w_recv.at[k], "row", sibling)
+    def weight_of(k, number=rows_n - 1, way=None):
+        place = others(weights[k], number * fw)
+        return remote(place, place, w_send.at[k], w_recv.at[k if way is None else way], "row", sibling)
+
+    if alike:
+        weight_of(0, twins - 1).wait_recv()
+    for twin in alike:
+        place = weights[0].at[pl.ds(pl.multiple_of(twin * fw, fw), fw)]
+        remote(place, place, w_send.at[0], w_recv.at[parts], "row", sibling).start()
 
     groups = rows_n // group
     strip = min(cut, 512)
@@ -270,7 +280,7 @@
     for part in range(cuts):
         turn_in(part)
         if part == 0:
-            weight_of(0).wait_recv()
+            weight_of(0, twins, parts).wait_recv()
         make(0, part)
         send_chunk(0, part)
     for h in range(1, split):
@@ -377,7 +387,7 @@
             dma((1,)),
             dma((cuts, feat // tile)),
             dma((parts,)),
-            dma((parts,)),
+            dma((parts + 1,)),
             dma((1,)),
             dma((chunks + cuts - 1, 2)),
             dma((1,)),

time: 103 us -> 102 us (level)
  no operation moved by 1% of the time
where the time goes in v5:
time: 102 us
  Pallas kernels  98.9 us (97%)
  local copies, waits for them, and re-layouts  2.26 us (2%)
    pallas_call x1, Pallas kernels, layer(): pl.pallas_call(functools.partial(layer_kernel, rows_n, parts), out_shape=...  98.9 us
    unnamed x1, local copies, waits for them, and re-layouts  2.26 us

profile of v5, /device:TPU:16, one launch (start us, length us, event | category | flops | bytes accessed | tf_op | source)
XLA Modules:
  0.0 101.8 jit_solution(17678784570665138305)
XLA Ops:
  0.7 98.9 %layer.1 = bf16[4096,128]{1,0:T(8,128)(2,1)} custom-call(s32[1]{0:T(128)S(6)} %copy.7.count_hbm, s32[2,256]{1,0:T(2,128)} %coords_hbm.1, bf16[64,8192]{1,0:T(8,128)(2,1)} %bitcast.2, bf16[64,512]{1,0:T(8,128)(2,1)} %bitcast.3, bf16[256,128,128]{2,1,0:T(8,128)(2,1)} %tiles_hbm.1), custom_call_target="tpu_custom_call" | custom-call | tf_op jit(solution)/shard_map/layer/pallas_call | solution.py:362
  99.5 2.3 %copy.8 = bf16[4096,128]{1,0:T(8,128)(2,1)} copy(bf16[4096,128]{1,0:T(8,128)(2,1)} %layer.1) | data formatting | bytes 2097152

commit v6 on v5

--- a/solution.py
+++ b/solution.py
@@ -218,22 +218,28 @@
             packed = jnp.concatenate([band[:cut // 2], band[cut // 2:]], axis=1)
             panels[k * split + h, pl.ds(me * whole + part * deep, deep)] = packed.reshape(deep, tile, tile)
 
+    def widen(c, at, part):
+        for cell in range(cuts) if part is None else (part,):
+            for i in range(deep):
+                both = panels[c, at * whole + cell * deep + i]
+                low = (at * cuts + cell) * 2 * deep + i
+                spread[low] = both
+                spread[low + deep] = jnp.concatenate([both[:, HALF:], both[:, :HALF]], axis=1)
+
     def collect(c, sections):
         for part in sections:
             awaited(c, part, twins - 1, 0)
-            for step in range(1, twins):
-                place = spot(c, lax.rem(me + 2 * step, rows_n), part)
+            for twin in alike:
+                place = spot(c, twin, part)
                 remote(place, place, sib_send.at[0], h_recv.at[line_of(c, part), 1], "row", sibling).start()
+            for twin in [me] + alike:
+                widen(c, twin, part)
         for part in sections:
             awaited(c, part, twins, 1)
+            for step in range(twins):
+                widen(c, lax.rem(sibling + 2 * step, rows_n), part)
 
     def multiply(c):
-        for at in range(rows_n * whole):
-            both = panels[c, at]
-            low = at // deep * 2 * deep + at % deep
-            spread[low] = both
-            spread[low + deep] = jnp.concatenate([both[:, HALF:], both[:, :HALF]], axis=1)
-
         def bunch(i, total):
             left, right = [], []
             for j in range(BUNCH):

time: 102 us -> 102 us (level)
  no operation moved by 1% of the time
where the time goes in v6:
time: 102 us
  Pallas kernels  98.9 us (97%)
  local copies, waits for them, and re-layouts  2.26 us (2%)
    pallas_call x1, Pallas kernels, layer(): pl.pallas_call(functools.partial(layer_kernel, rows_n, parts), out_shape=...  98.9 us
    unnamed x1, local copies, waits for them, and re-layouts  2.26 us

profile of v6, /device:TPU:16, one launch (start us, length us, event | category | flops | bytes accessed | tf_op | source)
XLA Modules:
  0.0 101.9 jit_solution(2848988099842213286)
XLA Ops:
  0.7 98.9 %layer.1 = bf16[4096,128]{1,0:T(8,128)(2,1)} custom-call(s32[1]{0:T(128)S(6)} %copy.7.count_hbm, s32[2,256]{1,0:T(2,128)} %coords_hbm.1, bf16[64,8192]{1,0:T(8,128)(2,1)} %bitcast.2, bf16[64,512]{1,0:T(8,128)(2,1)} %bitcast.3, bf16[256,128,128]{2,1,0:T(8,128)(2,1)} %tiles_hbm.1), custom_call_target="tpu_custom_call" | custom-call | tf_op jit(solution)/shard_map/layer/pallas_call | solution.py:368
  99.6 2.3 %copy.8 = bf16[4096,128]{1,0:T(8,128)(2,1)} copy(bf16[4096,128]{1,0:T(8,128)(2,1)} %layer.1) | data formatting | bytes 2097152
